TPU v7x, 32 devices: a whole 2x2x4 slice. The times are simulated.
32 devices in a mesh: src: 4 (over y, x), rcv: 8 (over z, core).
Axes of the slice: x: 2, y: 2, z: 4, core: 2. Of those that a mesh axis runs over, the one named last changes fastest.
Arguments:
- wavefield: float32 [2, 16, 2048, 2048], P(None, None, 'rcv', 'src')
- surface_band: float32 [2, 2048, 1024], P(None, 'rcv'), may hold values from -0.75 to 0.75
- band_shift: int32 [32], P('rcv'), may hold values from -16 to 16
- trace_mask: int32 [2048], P('rcv'), may hold values 0 or 1
- shot_taper: float32 [5], replicated, may hold values from 0.2 to 1
Outputs:
- multiples: float32 [2, 16, 2048, 2048], P(None, None, 'rcv', 'src')
- primaries: float32 [2, 16, 2048, 2048], P(None, None, 'rcv', 'src')
All inputs are finite; a program needn't handle non-finite values. No bound on the sum of `trace_mask` on one device may be relied on, other than what follows from the above.
Results may differ from a plain program's by a relative error of at most 0.0003.
Values sent between devices are 32-bit elements; how exact they have to be, the bound alone decides.
A program may use at most 192 MiB of HBM per device.

v0:
```python
import functools

import jax
import jax.numpy as jnp
from jax import lax
from jax.experimental import pallas as pl
from jax.experimental.pallas import tpu as pltpu
from jax.sharding import PartitionSpec as P

APER = 64
SHIFT = 16
BLOCK = 64
SHALF = 2
LANES = 128
HALO = APER // 2 + SHIFT
CHUNKS = 4
MESH = pl.DeviceIdType.MESH


def shifted(cells, axis, step):
    count = lax.axis_size(axis)
    ends = count - 1
    if step > 0:
        pairs = [(i, i + 1) for i in range(ends)]
    else:
        pairs = [(i + 1, i) for i in range(ends)]
    return lax.ppermute(cells, axis, pairs)


def split(cells):
    high = cells.astype(jnp.bfloat16)
    low = (cells - high.astype(jnp.float32)).astype(jnp.bfloat16)
    return high, low


def predict_kernel(first, shift_ref, taper_ref, wave_ref, mask_ref, above_ref, below_ref, side_ref, band_ref, *refs):
    mult_ref, energy_ref, rows_ref = refs[-3:]
    step = pl.program_id(0)
    here = first + step
    receivers, shots = wave_ref.shape[2:]
    width = shots + LANES

    data = jnp.float32(0)
    for x in range(2):
        wave = wave_ref[x, 0]
        data = data + jnp.sum(wave * wave)
        rows_ref[x, HALO : HALO + receivers, :shots] = wave * mask_ref[...]
        rows_ref[x, :HALO, :shots] = above_ref[x, 0]
        rows_ref[x, HALO + receivers : receivers + 2 * HALO, :shots] = below_ref[x, 0]
        rows_ref[x, : receivers + 2 * HALO, shots:] = side_ref[x, 0]

    odd = here % 2 == 1
    lane = lax.broadcasted_iota(jnp.int32, (BLOCK, LANES), 1)

    def skewed(x, index):
        taps = band_ref[x, index * BLOCK : (index + 1) * BLOCK, :]
        taps = jnp.where(odd, pltpu.roll(taps, LANES - APER, 1), taps)
        taps = jnp.where(lane < APER, taps, 0.0)
        return pltpu.roll(taps, 0, 1, stride=1, stride_axis=0)

    def near(x, whole, rest):
        tall = rows_ref[x, pl.ds(whole, 2 * BLOCK + 8), :]
        return pltpu.roll(tall, (2 * BLOCK + 8 - rest) % (2 * BLOCK + 8), 0)[: 2 * BLOCK]

    total = jnp.zeros((8, shots), jnp.float32)
    for index in range(receivers // BLOCK):
        start = index * BLOCK + HALO - APER // 2 + shift_ref[index]
        rest = start & 7
        whole = pl.multiple_of(start - rest, 8)
        window = jnp.concatenate([near(x, whole, rest) for x in range(2)], axis=0)
        high, low = split(window)
        real, imag = skewed(0, index), skewed(1, index)
        weights = jnp.concatenate(
            [jnp.concatenate([real, -imag], axis=1), jnp.concatenate([imag, real], axis=1)], axis=0
        )
        weights_high, weights_low = split(weights)
        both = jnp.concatenate([weights_high, weights_low], axis=0)
        upper = jnp.dot(both, high, preferred_element_type=jnp.float32)
        lower = jnp.dot(weights_high, low, preferred_element_type=jnp.float32)
        pred = upper[: 2 * BLOCK] + (upper[2 * BLOCK :] + lower)
        mult = taper_ref[SHALF] * pred[:, :shots]
        for u in range(2 * SHALF + 1):
            if u != SHALF:
                mult = mult + taper_ref[u] * pltpu.roll(pred, (SHALF - u) % width, 1)[:, :shots]
        mult_ref[0, 0, index * BLOCK : (index + 1) * BLOCK, :] = mult[:BLOCK]
        mult_ref[1, 0, index * BLOCK : (index + 1) * BLOCK, :] = mult[BLOCK:]
        total = total + jnp.sum((mult * mult).reshape(-1, 8, shots), axis=0)

    row = lax.broadcasted_iota(jnp.int32, (8, LANES), 0)
    col = lax.broadcasted_iota(jnp.int32, (8, LANES), 1)
    news = jnp.where(row == 0, data, jnp.sum(total))
    news = jnp.where((row < 2) & (col == here), news, 0.0)

    @pl.when(step == 0)
    def _():
        energy_ref[...] = jnp.zeros_like(energy_ref)

    energy_ref[...] += news


def predict(first, count, wave, mask, above, below, side, band, band_shift, shot_taper, mult):
    _, slices, receivers, shots = wave.shape
    in_specs = [
        pl.BlockSpec(memory_space=pltpu.SMEM),
        pl.BlockSpec(memory_space=pltpu.SMEM),
        pl.BlockSpec((2, 1, receivers, shots), lambda g: (0, first + g, 0, 0)),
        pl.BlockSpec((receivers, 1), lambda g: (0, 0)),
        pl.BlockSpec((2, 1, HALO, shots), lambda g: (0, g, 0, 0)),
        pl.BlockSpec((2, 1, HALO, shots), lambda g: (0, g, 0, 0)),
        pl.BlockSpec((2, 1, receivers + 2 * HALO, LANES), lambda g: (0, first + g, 0, 0)),
        pl.BlockSpec((2, receivers, LANES), lambda g: (0, 0, (first + g) // 2)),
    ]
    args = [band_shift, shot_taper, wave, mask, above, below, side, band]
    aliases = {}
    if mult is not None:
        in_specs.append(pl.BlockSpec(memory_space=pl.ANY))
        aliases = {len(args): 0}
        args.append(mult)
    flops = 3 * 2 * 4 * BLOCK * 4 * BLOCK * count * (receivers // BLOCK) * (shots + LANES)
    return pl.pallas_call(
        functools.partial(predict_kernel, first),
        grid=(count,),
        in_specs=in_specs,
        out_specs=[
            pl.BlockSpec((2, 1, receivers, shots), lambda g: (0, first + g, 0, 0)),
            pl.BlockSpec((8, LANES), lambda g: (0, 0)),
        ],
        out_shape=[
            jax.ShapeDtypeStruct(wave.shape, jnp.float32),
            jax.ShapeDtypeStruct((8, LANES), jnp.float32),
        ],
        scratch_shapes=[pltpu.VMEM((2, receivers + 2 * HALO + 8, shots + LANES), jnp.float32)],
        input_output_aliases=aliases,
        cost_estimate=pl.CostEstimate(
            flops=flops, bytes_accessed=count * receivers * shots * 20, transcendentals=0
        ),
        compiler_params=pltpu.CompilerParams(
            dimension_semantics=("arbitrary",), vmem_limit_bytes=48 * 2**20
        ),
        name=f"predict{first}",
    )(*args)


def gain_kernel(axes, *refs):
    energies, (gain_ref, mine, plane, space, local_sem, send_a, recv_a, send_b, recv_b) = refs[:-9], refs[-9:]
    (slow, slow_count), (fast, fast_count) = axes
    slow_me, fast_me = lax.axis_index(slow), lax.axis_index(fast)

    def slow_peer(d):
        return {slow: lax.rem(slow_me + d, slow_count)}

    def fast_peer(d):
        return {fast: lax.rem(fast_me + d, fast_count)}

    barrier = pltpu.get_barrier_semaphore()
    for d in range(1, slow_count):
        pl.semaphore_signal(barrier, inc=1, device_id=slow_peer(d), device_id_type=MESH)
    for d in range(1, fast_count):
        pl.semaphore_signal(barrier, inc=1, device_id=fast_peer(d), device_id_type=MESH)
    total = energies[0][...]
    for other in energies[1:]:
        total = total + other[...]
    mine[...] = total
    own = pltpu.make_async_copy(mine, plane.at[0], local_sem)
    own.start()
    pl.semaphore_wait(barrier, slow_count + fast_count - 2)

    copies = []
    for d in range(1, slow_count):
        copy = pltpu.make_async_remote_copy(
            src_ref=mine, dst_ref=plane.at[d], send_sem=send_a.at[d], recv_sem=recv_a.at[d],
            device_id=slow_peer(d), device_id_type=MESH,
        )
        copy.start()
        copies.append(copy)
    own.wait()
    for copy in copies:
        copy.wait()
    copies = []
    for d in range(1, fast_count):
        copy = pltpu.make_async_remote_copy(
            src_ref=plane, dst_ref=space.at[d - 1], send_sem=send_b.at[d], recv_sem=recv_b.at[d],
            device_id=fast_peer(d), device_id_type=MESH,
        )
        copy.start()
        copies.append(copy)
    total = jnp.sum(plane[...], axis=0)
    for copy in copies:
        copy.wait()
    for d in range(fast_count - 1):
        total = total + jnp.sum(space[d], axis=0)
    data = jnp.broadcast_to(total[0:1], total.shape)
    pred = jnp.broadcast_to(total[1:2], total.shape)
    gain_ref[...] = jnp.sqrt((data + 1e-06) / (pred + 1e-06))


def gains(energies, axes, identity):
    slow_count, fast_count = axes[0][1], axes[1][1]
    return pl.pallas_call(
        functools.partial(gain_kernel, axes),
        in_specs=[pl.BlockSpec(memory_space=pltpu.VMEM)] * len(energies),
        out_specs=pl.BlockSpec(memory_space=pltpu.VMEM),
        out_shape=jax.ShapeDtypeStruct((8, LANES), jnp.float32),
        scratch_shapes=[
            pltpu.VMEM((8, LANES), jnp.float32),
            pltpu.VMEM((slow_count, 8, LANES), jnp.float32),
            pltpu.VMEM((fast_count - 1, slow_count, 8, LANES), jnp.float32),
            pltpu.SemaphoreType.DMA,
            pltpu.SemaphoreType.DMA((slow_count,)),
            pltpu.SemaphoreType.DMA((slow_count,)),
            pltpu.SemaphoreType.DMA((fast_count,)),
            pltpu.SemaphoreType.DMA((fast_count,)),
        ],
        cost_estimate=pl.CostEstimate(flops=1000, bytes_accessed=8 * 2**20, transcendentals=0),
        compiler_params=pltpu.CompilerParams(collective_id=identity, has_side_effects=True),
        name=f"gains{identity}",
    )(*energies)


def subtract_kernel(first, gain_ref, wave_ref, mult_ref, *refs):
    prim_ref = refs[-1]
    here = first + pl.program_id(0)
    col = lax.broadcasted_iota(jnp.int32, (1, LANES), 1)
    gain = jnp.sum(jnp.where(col == here, gain_ref[0:1, :], 0.0))
    prim_ref[...] = wave_ref[...] - gain * mult_ref[...]


def subtract(first, count, gain, wave, mult, prim):
    _, slices, receivers, shots = wave.shape
    block = pl.BlockSpec((2, 1, receivers, shots), lambda g: (0, first + g, 0, 0))
    in_specs = [pl.BlockSpec((8, LANES), lambda g: (0, 0)), block, block]
    args = [gain, wave, mult]
    aliases = {}
    if prim is not None:
        in_specs.append(pl.BlockSpec(memory_space=pl.ANY))
        aliases = {len(args): 0}
        args.append(prim)
    return pl.pallas_call(
        functools.partial(subtract_kernel, first),
        grid=(count,),
        in_specs=in_specs,
        out_specs=block,
        out_shape=jax.ShapeDtypeStruct(wave.shape, jnp.float32),
        input_output_aliases=aliases,
        cost_estimate=pl.CostEstimate(
            flops=0, bytes_accessed=count * receivers * shots * 24, transcendentals=0
        ),
        compiler_params=pltpu.CompilerParams(
            dimension_semantics=("arbitrary",), vmem_limit_bytes=48 * 2**20
        ),
        name=f"subtract{first}",
    )(*args)


def per_device(wavefield, surface_band, band_shift, trace_mask, shot_taper):
    _, slices, receivers, shots = wavefield.shape
    mask = trace_mask.astype(jnp.float32)
    size = slices // CHUNKS

    halos = []
    for c in range(CHUNKS):
        part = wavefield[:, c * size : (c + 1) * size]
        tail = part[:, :, receivers - HALO :] * mask[None, None, receivers - HALO :, None]
        head = part[:, :, :HALO] * mask[None, None, :HALO, None]
        halos.append((shifted(tail, "rcv", 1), shifted(head, "rcv", -1)))

    first = jnp.swapaxes(wavefield[..., :SHALF] * mask[None, None, :, None], 2, 3)
    last = jnp.swapaxes(wavefield[..., shots - SHALF :] * mask[None, None, :, None], 2, 3)
    after = shifted(first, "src", -1)
    before = shifted(last, "src", 1)
    sides = jnp.concatenate([after, before], axis=2)
    sides = jnp.concatenate(
        [
            shifted(sides[..., receivers - HALO :], "rcv", 1),
            sides,
            shifted(sides[..., :HALO], "rcv", -1),
        ],
        axis=3,
    )
    gap = jnp.zeros((2, slices, LANES - 2 * SHALF, receivers + 2 * HALO), jnp.float32)
    side = jnp.swapaxes(jnp.concatenate([sides[:, :, :SHALF], gap, sides[:, :, SHALF:]], axis=2), 2, 3)

    column = mask[:, None]
    mult = None
    energies = []
    for c in range(CHUNKS):
        mult, energy = predict(
            c * size, size, wavefield, column, *halos[c], side, surface_band, band_shift, shot_taper, mult
        )
        energies.append(energy)
    axes = (("src", lax.axis_size("src")), ("rcv", lax.axis_size("rcv")))
    gain = gains(energies, axes, 1)
    prim = subtract(0, slices, gain, wavefield, mult, None)
    return (mult, prim)


def solution(mesh):
    in_specs = (P(None, None, "rcv", "src"), P(None, "rcv", None), P("rcv"), P("rcv"), P())
    out_specs = (P(None, None, "rcv", "src"), P(None, None, "rcv", "src"))
    return jax.shard_map(
        per_device, mesh=mesh, in_specs=in_specs, out_specs=out_specs, check_vma=False
    )
```

profile of v0, /device:TPU:0, one launch (start us, length us, event | category | flops | bytes accessed | tf_op | source)
XLA Modules:
  0.0 180.4 jit_solution(12440673070326086042)
XLA Ops:
  0.6 0.7 convert_element_type.3
  1.3 8.1 %fusion = (f32[2,16,256,2]{3,2,1,0:T(8,128)}, f32[2,16,256,2]{3,2,1,0:T(8,128)}) fusion(f32[2,16,256,512]{3,2,1,0:T(8,128)} %wave_ref.9), kind=kLoop, calls=%fused_computation.14 | loop fusion | bytes 262144 | tf_op jit(solution)/shard_map/slice | solution.py:268
  9.4 2.8 %copy.23 = f32[2,16,256,2]{2,1,3,0:T(8,128)S(1)} copy(f32[2,16,256,2]{3,2,1,0:T(8,128)} %get-tuple-element.30) | data formatting | bytes 131072
  12.3 2.8 %copy.22 = f32[2,16,256,2]{2,1,3,0:T(8,128)S(1)} copy(f32[2,16,256,2]{3,2,1,0:T(8,128)} %get-tuple-element.31) | data formatting | bytes 131072
  15.1 1.3 collective-permute-start.2
  16.4 0.1 fusion.3
  16.5 5.8 %slice_multiply_fusion = (f32[2,4,48,512]{3,2,1,0:T(8,128)}, f32[2,4,48,512]{3,2,1,0:T(8,128)}, f32[2,4,48,512]{3,2,1,0:T(8,128)}, f32[2,4,48,512]{3,2,1,0:T(8,1...) fusion(f32[2,16,256,512]{3,2,1,0:T(8,128)} %wave_ref.9, ...), kind=kLoop, calls=%fused_computation.1 | loop fusion | flops 1572864 | bytes 12583296 | tf_op jit(solution)/shard_map/mul | solution.py:264
  22.3 1.3 collective-permute-start.11
  23.6 1.3 collective-permute-start.9
  24.9 3.7 %collective-permute-start.10 = (f32[2,4,48,512]{3,2,1,0:T(8,128)}, f32[2,4,48,512]{3,2,1,0:T(8,128)S(1)}, u32[]{:S(2)}, u32[]{:S(2)}) collective-permute-start(f32[2,4,48,512]{3,2,1,0:T(8,128)} %get-tuple-element.29), channel_id=1, source_target_pairs={{0,1},{1,2},{2,3},{3,4},{4,5},{5,6},{6,7},{8,9},{9,10},{10,11},{11... | collective-permute-start | bytes 2359304 | tf_op jit(solution)/shard_map/ppermute | solution.py:27
  28.6 5.5 %collective-permute-start.3 = (f32[2,16,2,256]{3,1,2,0:T(8,128)S(1)}, f32[2,16,2,256]{3,1,2,0:T(8,128)S(1)}, u32[]{:S(2)}, u32[]{:S(2)}) collective-permute-start(f32[2,16,2,256]{3,1,2,0:T(8,128)S(1)} %get-tuple-element.36), channel_id=1, source_target_pairs={{0,8},{8,16},{16,24},{1,9},{9,17},{17,25},{2,10},{10,18},{18,26},{... | collective-permute-start | bytes 196616 | tf_op jit(solution)/shard_map/ppermute | solution.py:27
  34.1 0.0 collective-permute-done.2
  34.2 1.9 %collective-permute-done.3 = f32[2,16,2,256]{3,1,2,0:T(8,128)S(1)} collective-permute-done((f32[2,16,2,256]{3,1,2,0:T(8,128)S(1)}, f32[2,16,2,256]{3,1,2,0:T(8,128)S(1)}, u32[]{:S(2)}, u32[]{:S(2)}) %collective-permute-start.3) | collective-permute-done | bytes 65568 | tf_op jit(solution)/shard_map/ppermute | solution.py:27
  36.0 0.6 fusion.2
  36.7 2.7 %collective-permute-start.4 = (f32[2,16,4,48]{3,1,2,0:T(8,128)S(1)}, f32[2,16,4,48]{3,1,2,0:T(8,128)S(1)}, u32[]{:S(2)}, u32[]{:S(2)}) collective-permute-start(f32[2,16,4,48]{3,1,2,0:T(8,128)S(1)} %get-tuple-element.34), channel_id=1, source_target_pairs={{0,1},{1,2},{2,3},{3,4},{4,5},{5,6},{6,7},{8,9},{9,10},{10,11},{11... | collective-permute-start | bytes 73736 | tf_op jit(solution)/shard_map/ppermute | solution.py:27
  39.4 1.3 collective-permute-start.5
  40.7 0.1 copy.21.mask_ref
  40.9 0.1 pad.1.clone
  40.9 0.0 collective-permute-done.4
  40.9 1.3 collective-permute-start.7
  42.2 1.4 collective-permute-done.5
  43.6 5.7 %collective-permute-start.8 = (f32[2,4,48,512]{3,2,1,0:T(8,128)}, f32[2,4,48,512]{3,2,1,0:T(8,128)}, u32[]{:S(2)}, u32[]{:S(2)}) collective-permute-start(f32[2,4,48,512]{3,2,1,0:T(8,128)} %get-tuple-element.28), channel_id=1, source_target_pairs={{0,1},{1,2},{2,3},{3,4},{4,5},{5,6},{6,7},{8,9},{9,10},{10,11},{11... | collective-permute-start | bytes 2359304 | tf_op jit(solution)/shard_map/ppermute | solution.py:27
  49.3 0.1 pad_maximum_fusion
  49.5 3.4 %copy.16 = f32[2,16,2,352]{2,3,1,0:T(8,128)} copy(f32[2,16,2,352]{3,1,2,0:T(8,128)S(1)} %get-tuple-element.32) | data formatting | bytes 180224 | tf_op jit(solution)/shard_map/slice | solution.py:281
  52.9 3.4 %copy.17 = f32[2,16,2,352]{2,3,1,0:T(8,128)} copy(f32[2,16,2,352]{3,1,2,0:T(8,128)S(1)} %get-tuple-element.33) | data formatting | bytes 180224 | tf_op jit(solution)/shard_map/slice | solution.py:281
  56.3 0.0 collective-permute-done.11.below_ref
  56.3 0.0 copy-start.9
  56.3 0.0 copy-start.8
  56.3 0.0 copy-start
  56.3 0.0 copy-start.2
  56.3 0.0 copy-start.3
  56.4 1.6 collective-permute-start.6
  58.0 8.4 %maximum_bitcast_fusion.side_ref = f32[2,16,352,128]{3,2,1,0:T(8,128)} fusion(f32[2,16,2,352]{2,3,1,0:T(8,128)} %copy.17, f32[2,16,2,352]{2,3,1,0:T(8,128)} %copy.16, f32[128]{0:T(128)S(1)} %pad.1.clone), kind=kLoop, calls=%fused_computation | loop fusion | flops 2883584 | bytes 5947904 | tf_op jit(solution)/shard_map/transpose | solution.py:281
  66.4 0.0 collective-permute-done.9.below_ref
  66.4 0.0 copy-done.9
  66.4 1.3 collective-permute-start.1
  67.7 0.0 collective-permute-done.10.above_ref
  67.7 0.0 copy-done.8
  67.7 4.2 %collective-permute-start = (f32[2,4,48,512]{3,2,1,0:T(8,128)S(1)}, f32[2,4,48,512]{3,2,1,0:T(8,128)S(1)}, u32[]{:S(2)}, u32[]{:S(2)}) collective-permute-start(f32[2,4,48,512]{3,2,1,0:T(8,128)S(1)} %copy-done.8), channel_id=1, source_target_pairs={{0,1},{1,2},{2,3},{3,4},{4,5},{5,6},{6,7},{8,9},{9,10},{10,11},{11... | collective-permute-start | bytes 2359304 | tf_op jit(solution)/shard_map/ppermute | solution.py:27
  71.9 0.0 copy-done
  71.9 0.0 copy-done.2
  71.9 0.0 copy-done.3
  71.9 17.4 %predict0.1 = (f32[2,16,256,512]{3,2,1,0:T(8,128)}, f32[8,128]{1,0:T(8,128)S(1)}) custom-call(s32[4]{0:T(128)S(1)} %copy-done.2, f32[5]{0:T(128)S(1)} %copy-done.3, f32[2,16,256,512]{3,2,1,0:T(8,128)} %wave_ref.9, f32[256,1]{1,0:T(8,128)S(1)} %copy.21.mask_ref, f32[2,4,48,512]{3,2,1,0:T(8,128)S(1)} %collective-permute-done.10.above_ref, ...), custom_call_target="tpu_custom_call" | custom-call | flops 4026531840 | bytes 10485760 | tf_op jit(solution)/shard_map/predict0/pallas_call | solution.py:120
  89.3 0.0 copy-start.4
  89.3 0.0 collective-permute-done.8.above_ref
  89.3 17.5 %predict4.1 = (f32[2,16,256,512]{3,2,1,0:T(8,128)}, f32[8,128]{1,0:T(8,128)S(1)}) custom-call(s32[4]{0:T(128)S(1)} %copy-done.2, f32[5]{0:T(128)S(1)} %copy-done.3, f32[2,16,256,512]{3,2,1,0:T(8,128)} %wave_ref.9, f32[256,1]{1,0:T(8,128)S(1)} %copy.21.mask_ref, f32[2,4,48,512]{3,2,1,0:T(8,128)} %collective-permute-done.8.above_ref, ...), custom_call_target="tpu_custom_call", output_to_operand_aliasing={{0}: (8, {})} | custom-call | flops 4026531840 | bytes 10485760 | tf_op jit(solution)/shard_map/predict4/pallas_call | solution.py:120
  106.8 0.0 copy-done.4
  106.8 0.0 copy-start.5
  106.8 0.6 copy-done.5
  107.4 0.0 collective-permute-done.7.below_ref
  107.4 0.0 collective-permute-done.6.above_ref
  107.4 17.4 %predict8.1 = (f32[2,16,256,512]{3,2,1,0:T(8,128)}, f32[8,128]{1,0:T(8,128)S(1)}) custom-call(s32[4]{0:T(128)S(1)} %copy-done.2, f32[5]{0:T(128)S(1)} %copy-done.3, f32[2,16,256,512]{3,2,1,0:T(8,128)} %wave_ref.9, f32[256,1]{1,0:T(8,128)S(1)} %copy.21.mask_ref, ...), custom_call_target="tpu_custom_call", output_to_operand_aliasing={{0}: (8, {})} | custom-call | flops 4026531840 | bytes 10485760 | tf_op jit(solution)/shard_map/predict8/pallas_call | solution.py:120
  124.8 0.0 copy-start.6
  124.8 0.0 collective-permute-done.1.below_ref
  124.8 0.0 collective-permute-done.above_ref
  124.8 17.6 %predict12.1 = (f32[2,16,256,512]{3,2,1,0:T(8,128)}, f32[8,128]{1,0:T(8,128)S(1)}) custom-call(s32[4]{0:T(128)S(1)} %copy-done.2, f32[5]{0:T(128)S(1)} %copy-done.3, f32[2,16,256,512]{3,2,1,0:T(8,128)} %wave_ref.9, f32[256,1]{1,0:T(8,128)S(1)} %copy.21.mask_ref, ...), custom_call_target="tpu_custom_call", output_to_operand_aliasing={{0}: (8, {})} | custom-call | flops 4026531840 | bytes 10485760 | tf_op jit(solution)/shard_map/predict12/pallas_call | solution.py:120
  142.5 0.0 copy-done.6
  142.5 0.0 copy-start.7
  142.5 0.6 copy-done.7
  143.0 14.5 %gains1.1.gain_ref = f32[8,128]{1,0:T(8,128)} custom-call(f32[8,128]{1,0:T(8,128)} %copy-done.4, f32[8,128]{1,0:T(8,128)} %copy-done.5, f32[8,128]{1,0:T(8,128)} %copy-done.6, f32[8,128]{1,0:T(8,128)} %copy-done.7), custom_call_target="tpu_custom_call" | custom-call | flops 1000 | bytes 8388608 | tf_op jit(solution)/shard_map/gains1/pallas_call | solution.py:199
  157.5 0.0 copy-start.1
  157.5 0.7 copy-done.1
  158.2 22.2 %subtract0.1 = f32[2,16,256,512]{3,2,1,0:T(8,128)} custom-call(f32[8,128]{1,0:T(8,128)S(1)} %copy-done.1, f32[2,16,256,512]{3,2,1,0:T(8,128)} %wave_ref.9, f32[2,16,256,512]{3,2,1,0:T(8,128)} %get-tuple-element.8.mult_ref), custom_call_target="tpu_custom_call" | custom-call | bytes 50331648 | tf_op jit(solution)/shard_map/subtract0/pallas_call | solution.py:238
  (5 shorter events, 0.1 us)
Async XLA Ops:
  15.1 19.0 %collective-permute-start.2 = (f32[2,16,2,256]{3,1,2,0:T(8,128)S(1)}, f32[2,16,2,256]{3,1,2,0:T(8,128)S(1)}, u32[]{:S(2)}, u32[]{:S(2)}) collective-permute-start(f32[2,16,2,256]{3,1,2,0:T(8,128)S(1)} %get-tuple-element.37), channel_id=1, source_target_pairs={{8,0},{16,8},{24,16},{9,1},{17,9},{25,17},{10,2},{18,10},{26,18},{... | collective-permute-start | bytes 196616 | tf_op jit(solution)/shard_map/ppermute | solution.py:27
  22.3 34.0 %collective-permute-start.11 = (f32[2,4,48,512]{3,2,1,0:T(8,128)}, f32[2,4,48,512]{3,2,1,0:T(8,128)S(1)}, u32[]{:S(2)}, u32[]{:S(2)}) collective-permute-start(f32[2,4,48,512]{3,2,1,0:T(8,128)} %get-tuple-element.18), channel_id=1, source_target_pairs={{1,0},{2,1},{3,2},{4,3},{5,4},{6,5},{7,6},{9,8},{10,9},{11,10},{12... | collective-permute-start | bytes 2359304 | tf_op jit(solution)/shard_map/ppermute | solution.py:27
  23.6 42.8 %collective-permute-start.9 = (f32[2,4,48,512]{3,2,1,0:T(8,128)}, f32[2,4,48,512]{3,2,1,0:T(8,128)S(1)}, u32[]{:S(2)}, u32[]{:S(2)}) collective-permute-start(f32[2,4,48,512]{3,2,1,0:T(8,128)} %get-tuple-element.19), channel_id=1, source_target_pairs={{1,0},{2,1},{3,2},{4,3},{5,4},{6,5},{7,6},{9,8},{10,9},{11,10},{12... | collective-permute-start | bytes 2359304 | tf_op jit(solution)/shard_map/ppermute | solution.py:27
  24.9 42.8 %collective-permute-start.10 = (f32[2,4,48,512]{3,2,1,0:T(8,128)}, f32[2,4,48,512]{3,2,1,0:T(8,128)S(1)}, u32[]{:S(2)}, u32[]{:S(2)}) collective-permute-start(f32[2,4,48,512]{3,2,1,0:T(8,128)} %get-tuple-element.29), channel_id=1, source_target_pairs={{0,1},{1,2},{2,3},{3,4},{4,5},{5,6},{6,7},{8,9},{9,10},{10,11},{11... | collective-permute-start | bytes 2359304 | tf_op jit(solution)/shard_map/ppermute | solution.py:27
  28.6 7.4 %collective-permute-start.3 = (f32[2,16,2,256]{3,1,2,0:T(8,128)S(1)}, f32[2,16,2,256]{3,1,2,0:T(8,128)S(1)}, u32[]{:S(2)}, u32[]{:S(2)}) collective-permute-start(f32[2,16,2,256]{3,1,2,0:T(8,128)S(1)} %get-tuple-element.36), channel_id=1, source_target_pairs={{0,8},{8,16},{16,24},{1,9},{9,17},{17,25},{2,10},{10,18},{18,26},{... | collective-permute-start | bytes 196616 | tf_op jit(solution)/shard_map/ppermute | solution.py:27
  36.7 4.3 %collective-permute-start.4 = (f32[2,16,4,48]{3,1,2,0:T(8,128)S(1)}, f32[2,16,4,48]{3,1,2,0:T(8,128)S(1)}, u32[]{:S(2)}, u32[]{:S(2)}) collective-permute-start(f32[2,16,4,48]{3,1,2,0:T(8,128)S(1)} %get-tuple-element.34), channel_id=1, source_target_pairs={{0,1},{1,2},{2,3},{3,4},{4,5},{5,6},{6,7},{8,9},{9,10},{10,11},{11... | collective-permute-start | bytes 73736 | tf_op jit(solution)/shard_map/ppermute | solution.py:27
  39.4 4.2 %collective-permute-start.5 = (f32[2,16,4,48]{3,1,2,0:T(8,128)}, f32[2,16,4,48]{3,1,2,0:T(8,128)S(1)}, u32[]{:S(2)}, u32[]{:S(2)}) collective-permute-start(f32[2,16,4,48]{3,1,2,0:T(8,128)} %get-tuple-element.35), channel_id=1, source_target_pairs={{1,0},{2,1},{3,2},{4,3},{5,4},{6,5},{7,6},{9,8},{10,9},{11,10},{12... | collective-permute-start | bytes 73736 | tf_op jit(solution)/shard_map/ppermute | solution.py:27
  40.9 66.5 %collective-permute-start.7 = (f32[2,4,48,512]{3,2,1,0:T(8,128)}, f32[2,4,48,512]{3,2,1,0:T(8,128)S(1)}, u32[]{:S(2)}, u32[]{:S(2)}) collective-permute-start(f32[2,4,48,512]{3,2,1,0:T(8,128)} %get-tuple-element.20), channel_id=1, source_target_pairs={{1,0},{2,1},{3,2},{4,3},{5,4},{6,5},{7,6},{9,8},{10,9},{11,10},{12... | collective-permute-start | bytes 2359304 | tf_op jit(solution)/shard_map/ppermute | solution.py:27
  43.6 45.7 %collective-permute-start.8 = (f32[2,4,48,512]{3,2,1,0:T(8,128)}, f32[2,4,48,512]{3,2,1,0:T(8,128)}, u32[]{:S(2)}, u32[]{:S(2)}) collective-permute-start(f32[2,4,48,512]{3,2,1,0:T(8,128)} %get-tuple-element.28), channel_id=1, source_target_pairs={{0,1},{1,2},{2,3},{3,4},{4,5},{5,6},{6,7},{8,9},{9,10},{10,11},{11... | collective-permute-start | bytes 2359304 | tf_op jit(solution)/shard_map/ppermute | solution.py:27
  56.3 10.0 %copy-start.9 = (f32[2,4,48,512]{3,2,1,0:T(8,128)S(1)}, f32[2,4,48,512]{3,2,1,0:T(8,128)}, u32[]{:S(2)}) copy-start(f32[2,4,48,512]{3,2,1,0:T(8,128)} %get-tuple-element.21) | copy-start | bytes 2359300
  56.3 11.3 %copy-start.8 = (f32[2,4,48,512]{3,2,1,0:T(8,128)S(1)}, f32[2,4,48,512]{3,2,1,0:T(8,128)}, u32[]{:S(2)}) copy-start(f32[2,4,48,512]{3,2,1,0:T(8,128)} %get-tuple-element.26) | copy-start | bytes 2359300
  56.3 15.6 %copy-start = (f32[2,256,1024]{2,1,0:T(8,128)S(1)}, f32[2,256,1024]{2,1,0:T(8,128)}, u32[]{:S(2)}) copy-start(f32[2,256,1024]{2,1,0:T(8,128)} %band_ref.7) | copy-start | bytes 6291460
  56.3 15.6 %copy-start.2 = (s32[4]{0:T(128)S(1)}, s32[4]{0:T(128)}, u32[]{:S(2)}) copy-start(s32[4]{0:T(128)} %shift_ref.7) | copy-start | bytes 52
  56.3 15.6 %copy-start.3 = (f32[5]{0:T(128)S(1)}, f32[5]{0:T(128)}, u32[]{:S(2)}) copy-start(f32[5]{0:T(128)} %taper_ref.7) | copy-start | bytes 64
  56.4 51.0 %collective-permute-start.6 = (f32[2,4,48,512]{3,2,1,0:T(8,128)}, f32[2,4,48,512]{3,2,1,0:T(8,128)S(1)}, u32[]{:S(2)}, u32[]{:S(2)}) collective-permute-start(f32[2,4,48,512]{3,2,1,0:T(8,128)} %get-tuple-element.27), channel_id=1, source_target_pairs={{0,1},{1,2},{2,3},{3,4},{4,5},{5,6},{6,7},{8,9},{9,10},{10,11},{11... | collective-permute-start | bytes 2359304 | tf_op jit(solution)/shard_map/ppermute | solution.py:27
  66.4 58.4 %collective-permute-start.1 = (f32[2,4,48,512]{3,2,1,0:T(8,128)S(1)}, f32[2,4,48,512]{3,2,1,0:T(8,128)S(1)}, u32[]{:S(2)}, u32[]{:S(2)}) collective-permute-start(f32[2,4,48,512]{3,2,1,0:T(8,128)S(1)} %copy-done.9), channel_id=1, source_target_pairs={{1,0},{2,1},{3,2},{4,3},{5,4},{6,5},{7,6},{9,8},{10,9},{11,10},{12... | collective-permute-start | bytes 2359304 | tf_op jit(solution)/shard_map/ppermute | solution.py:27
  67.7 57.1 %collective-permute-start = (f32[2,4,48,512]{3,2,1,0:T(8,128)S(1)}, f32[2,4,48,512]{3,2,1,0:T(8,128)S(1)}, u32[]{:S(2)}, u32[]{:S(2)}) collective-permute-start(f32[2,4,48,512]{3,2,1,0:T(8,128)S(1)} %copy-done.8), channel_id=1, source_target_pairs={{0,1},{1,2},{2,3},{3,4},{4,5},{5,6},{6,7},{8,9},{9,10},{10,11},{11... | collective-permute-start | bytes 2359304 | tf_op jit(solution)/shard_map/ppermute | solution.py:27
  89.3 17.5 %copy-start.4 = (f32[8,128]{1,0:T(8,128)}, f32[8,128]{1,0:T(8,128)S(1)}, u32[]{:S(2)}) copy-start(f32[8,128]{1,0:T(8,128)S(1)} %get-tuple-element.14.refs_0_) | copy-start | bytes 12292
  106.8 0.6 copy-start.5
  124.8 17.7 %copy-start.6 = (f32[8,128]{1,0:T(8,128)}, f32[8,128]{1,0:T(8,128)S(1)}, u32[]{:S(2)}) copy-start(f32[8,128]{1,0:T(8,128)S(1)} %get-tuple-element.16.refs_2_) | copy-start | bytes 12292
  142.5 0.6 copy-start.7
  157.5 0.7 copy-start.1
where the time goes:
time: 181 us; the launch traced here: 180 us
  Pallas kernels  107 us (59%)
  starting transfers between devices  31.2 us (17%)
  local copies, waits for them, and re-layouts  23.4 us (13%)
  other arithmetic  15 us (8%)
  waiting for transfers between devices  3.26 us (2%)
    pallas_call x4, Pallas kernels, predict(): pl.pallas_call(functools.partial(predict_kernel, first), grid=(count,), i...  69.9 us
    ppermute x12, starting transfers between devices, shifted(): return lax.ppermute(cells, axis, pairs)  31.2 us
    pallas_call x1, Pallas kernels, subtract(): pl.pallas_call(functools.partial(subtract_kernel, first), grid=(count,),...  22.2 us
    pallas_call x1, Pallas kernels, gains(): pl.pallas_call(functools.partial(gain_kernel, axes), in_specs=[pl.BlockSp...  14.5 us
    transpose x1, other arithmetic, per_device(): jnp.swapaxes(jnp.concatenate([sides[:, :, :SHALF], gap, sides[:, :, SHALF...  8.39 us
    slice x1, local copies, waits for them, and re-layouts, per_device(): wavefield[..., shots - SHALF:] * mask[None, None, :, None]  8.11 us
    unnamed x23, local copies, waits for them, and re-layouts  7.57 us
    mul x1, other arithmetic, per_device(): head = part[:, :, :HALO] * mask[None, None, :HALO, None]  5.82 us
  transfers between devices with their start and end apart: 12, of which 2 were waited for; matrix products, arithmetic and copies ran while one was open for 12% of the time, Pallas kernels for 29%

commit v1 on v0

--- a/solution.py
+++ b/solution.py
@@ -13,7 +13,7 @@
 SHALF = 2
 LANES = 128
 HALO = APER // 2 + SHIFT
-CHUNKS = 4
+CHUNKS = 2
 MESH = pl.DeviceIdType.MESH
 
 
@@ -264,8 +264,10 @@
         head = part[:, :, :HALO] * mask[None, None, :HALO, None]
         halos.append((shifted(tail, "rcv", 1), shifted(head, "rcv", -1)))
 
-    first = jnp.swapaxes(wavefield[..., :SHALF] * mask[None, None, :, None], 2, 3)
-    last = jnp.swapaxes(wavefield[..., shots - SHALF :] * mask[None, None, :, None], 2, 3)
+    pick = jnp.eye(SHALF, LANES, dtype=jnp.float32)
+    turn = functools.partial(jnp.einsum, precision=lax.Precision.HIGHEST)
+    first = turn("cl,xfrl->xfcr", pick, wavefield[..., :LANES]) * mask
+    last = turn("cl,xfrl->xfcr", jnp.roll(pick, -SHALF, 1), wavefield[..., shots - LANES :]) * mask
     after = shifted(first, "src", -1)
     before = shifted(last, "src", 1)
     sides = jnp.concatenate([after, before], axis=2)
@@ -277,9 +279,8 @@
         ],
         axis=3,
     )
-    gap = jnp.zeros((2, slices, LANES - 2 * SHALF, receivers + 2 * HALO), jnp.float32)
-    side = jnp.swapaxes(jnp.concatenate([sides[:, :, :SHALF], gap, sides[:, :, SHALF:]], axis=2), 2, 3)
-
+    place = jnp.concatenate([pick, jnp.roll(pick, -SHALF, 1)], axis=0)
+    side = turn("xfcr,cl->xfrl", sides, place)
     column = mask[:, None]
     mult = None
     energies = []

time: 181 us -> 168 us (0.928)
  local copies, waits for them, and re-layouts: 23.4 us -> 1.56 us
  matrix products: 0 us -> 21.3 us
  starting transfers between devices: 31.2 us -> 20.6 us
  waiting for transfers between devices: 3.26 us -> 13.4 us
  other arithmetic: 15 us -> 7.68 us
  Pallas kernels: 107 us -> 102 us
    dot_general x0 -> x3, matrix products: none -> 21.3 us  [the longest x1 11.4 us: per_device(): side = turn('xfcr,cl->xfrl', sides, place)]
    slice x5 -> x1, local copies, waits for them, and re-layouts: 15.6 us -> 0.07 us  [per_device(): jnp.roll(pick, -SHALF, 1)]
    ppermute x12 -> x8, starting transfers between devices: 31.2 us -> 20.6 us  [shifted(): return lax.ppermute(cells, axis, pairs)]
    ppermute x12 -> x8, waiting for transfers between devices: 3.26 us -> 13.4 us  [shifted(): return lax.ppermute(cells, axis, pairs)]
    transpose x2 -> x0, other arithmetic: 8.41 us -> none  [the longest x1 8.39 us: per_device(): jnp.swapaxes(jnp.concatenate([sides[:, :, :SHALF], gap, sides[:, :, SHALF...]
    unnamed x23 -> x12, local copies, waits for them, and re-layouts: 7.57 us -> 1.28 us
    pallas_call x4 -> x2, Pallas kernels: 69.9 us -> 65.4 us  [predict(): pl.pallas_call(functools.partial(predict_kernel, first), grid=(count,), i...]
  transfers between devices with their start and end apart: 12 -> 8, of which waited for: 2 -> 3; matrix products, arithmetic and copies ran while one was open for 12% -> 13% of each run, Pallas kernels for 29% -> 19%
where the time goes in v1:
time: 168 us
  Pallas kernels  102 us (61%)
  matrix products  21.3 us (13%)
  starting transfers between devices  20.6 us (12%)
  waiting for transfers between devices  13.4 us (8%)
  other arithmetic  7.68 us (5%)
    pallas_call x2, Pallas kernels, predict(): pl.pallas_call(functools.partial(predict_kernel, first), grid=(count,), i...  65.4 us
    pallas_call x1, Pallas kernels, subtract(): pl.pallas_call(functools.partial(subtract_kernel, first), grid=(count,),...  22.2 us
    ppermute x8, starting transfers between devices, shifted(): return lax.ppermute(cells, axis, pairs)  20.6 us
    pallas_call x1, Pallas kernels, gains(): pl.pallas_call(functools.partial(gain_kernel, axes), in_specs=[pl.BlockSp...  14.7 us
    ppermute x8, waiting for transfers between devices, shifted(): return lax.ppermute(cells, axis, pairs)  13.4 us
    dot_general x1, matrix products, per_device(): side = turn('xfcr,cl->xfrl', sides, place)  11.4 us
    mul x1, other arithmetic, per_device(): head = part[:, :, :HALO] * mask[None, None, :HALO, None]  6.27 us
    dot_general x1, matrix products, per_device(): turn('cl,xfrl->xfcr', jnp.roll(pick, -SHALF, 1), wavefield[..., shots - L...  5.66 us
  transfers between devices with their start and end apart: 8, of which 3 were waited for; matrix products, arithmetic and copies ran while one was open for 13% of the time, Pallas kernels for 19%

profile of v1, /device:TPU:0, one launch (start us, length us, event | category | flops | bytes accessed | tf_op | source)
XLA Modules:
  0.0 167.7 jit_solution(1379211558326909645)
XLA Ops:
  0.6 0.7 convert_element_type.10
  1.3 0.1 fusion.35
  1.4 6.3 %slice_multiply_fusion = (f32[2,8,48,512]{3,2,1,0:T(8,128)}, f32[2,8,48,512]{3,2,1,0:T(8,128)}, f32[2,8,48,512]{3,2,1,0:T(8,128)}, f32[2,8,48,512]{3,2,1,0:T(8,128)}) fusion(f32[2,16,256,512]{3,2,1,0:T(8,128)} %wave_ref.5, f32[48]{0:T(128)S(1)} %get-tuple-element.18, f32[48]{0:T(128)S(1)} %get-tuple-element.19), kind=kLoop, calls=%fused_computation.4 | loop fusion | flops 1572864 | bytes 12583296 | tf_op jit(solution)/shard_map/mul | solution.py:264
  7.7 1.3 collective-permute-start.7
  8.9 4.2 %collective-permute-start.6 = (f32[2,8,48,512]{3,2,1,0:T(8,128)}, f32[2,8,48,512]{3,2,1,0:T(8,128)}, u32[]{:S(2)}, u32[]{:S(2)}) collective-permute-start(f32[2,8,48,512]{3,2,1,0:T(8,128)} %get-tuple-element.15), channel_id=1, source_target_pairs={{0,1},{1,2},{2,3},{3,4},{4,5},{5,6},{6,7},{8,9},{9,10},{10,11},{11... | collective-permute-start | bytes 4718600 | tf_op jit(solution)/shard_map/ppermute | solution.py:27
  13.2 4.2 %fusion.7 = f32[2,16,2,256]{3,2,1,0:T(2,128)S(1)} fusion(f32[2,16,256,512]{3,2,1,0:T(8,128)} %wave_ref.5, f32[256]{0:T(256)S(1)} %convert_element_type.10), kind=kOutput, calls=%fused_computation.9 | convolution fusion | flops 25182464 | bytes 4260864 | tf_op jit(solution)/shard_map/cl,xfrl->xfcr/dot_general | solution.py:269
  17.4 1.3 collective-permute-start.2
  18.7 1.3 collective-permute-start.1
  20.0 4.1 %collective-permute-start = (f32[2,8,48,512]{3,2,1,0:T(8,128)}, f32[2,8,48,512]{3,2,1,0:T(8,128)S(1)}, u32[]{:S(2)}, u32[]{:S(2)}) collective-permute-start(f32[2,8,48,512]{3,2,1,0:T(8,128)} %get-tuple-element.14), channel_id=1, source_target_pairs={{0,1},{1,2},{2,3},{3,4},{4,5},{5,6},{6,7},{8,9},{9,10},{10,11},{11... | collective-permute-start | bytes 4718600 | tf_op jit(solution)/shard_map/ppermute | solution.py:27
  24.1 0.1 slice.53
  24.2 5.7 %fusion.13 = f32[2,16,2,256]{3,2,1,0:T(2,128)S(1)} fusion(f32[2,16,256,512]{3,2,1,0:T(8,128)} %wave_ref.5, f32[256]{0:T(256)S(1)} %convert_element_type.10, f32[2,2]{1,0:T(2,128)S(1)} %bitcast.22, f32[2,126]{1,0:T(2,128)S(1)} %slice.53), kind=kOutput, calls=%fused_computation.11 | convolution fusion | flops 25182464 | bytes 4261888 | tf_op jit(solution)/shard_map/cl,xfrl->xfcr/dot_general | solution.py:270
  29.8 0.0 collective-permute-done.2
  29.8 4.5 %collective-permute-start.3 = (f32[2,16,2,256]{3,2,1,0:T(2,128)S(1)}, f32[2,16,2,256]{3,2,1,0:T(2,128)S(1)}, u32[]{:S(2)}, u32[]{:S(2)}) collective-permute-start(f32[2,16,2,256]{3,2,1,0:T(2,128)S(1)} %fusion.13), channel_id=1, source_target_pairs={{0,8},{8,16},{16,24},{1,9},{9,17},{17,25},{2,10},{10,18},{18,26},{... | collective-permute-start | bytes 196616 | tf_op jit(solution)/shard_map/ppermute | solution.py:27
  34.4 2.1 %collective-permute-done.3 = f32[2,16,2,256]{3,2,1,0:T(2,128)S(1)} collective-permute-done((f32[2,16,2,256]{3,2,1,0:T(2,128)S(1)}, f32[2,16,2,256]{3,2,1,0:T(2,128)S(1)}, u32[]{:S(2)}, u32[]{:S(2)}) %collective-permute-start.3) | collective-permute-done | bytes 65568 | tf_op jit(solution)/shard_map/ppermute | solution.py:27
  36.4 0.7 fusion.24
  37.2 2.4 %collective-permute-start.4 = (f32[2,16,4,48]{3,2,1,0:T(4,128)S(1)}, f32[2,16,4,48]{3,2,1,0:T(4,128)S(1)}, u32[]{:S(2)}, u32[]{:S(2)}) collective-permute-start(f32[2,16,4,48]{3,2,1,0:T(4,128)S(1)} %get-tuple-element.16), channel_id=1, source_target_pairs={{0,1},{1,2},{2,3},{3,4},{4,5},{5,6},{6,7},{8,9},{9,10},{10,11},{11... | collective-permute-start | bytes 73736 | tf_op jit(solution)/shard_map/ppermute | solution.py:27
  39.6 0.9 collective-permute-done.4
  40.5 1.5 collective-permute-start.5
  41.9 0.1 copy.9.mask_ref
  42.1 0.0 copy-start
  42.1 0.0 copy-start.4
  42.1 0.0 copy-start.5
  42.1 10.5 %collective-permute-done.5 = f32[2,16,4,48]{3,2,1,0:T(4,128)S(1)} collective-permute-done((f32[2,16,4,48]{3,2,1,0:T(4,128)}, f32[2,16,4,48]{3,2,1,0:T(4,128)S(1)}, u32[]{:S(2)}, u32[]{:S(2)}) %collective-permute-start.5) | collective-permute-done | bytes 24608 | tf_op jit(solution)/shard_map/ppermute | solution.py:27
  52.6 11.4 %fusion.16.side_ref = f32[2,16,352,128]{3,2,1,0:T(8,128)} fusion(f32[2,16,4,48]{3,2,1,0:T(4,128)S(1)} %collective-permute-done.5, f32[2,16,2,256]{3,2,1,0:T(2,128)S(1)} %collective-permute-done.3, f32[2,16,2,256]{3,2,1,0:T(2,128)S(1)} %collective-permute-done.2, f32[2,16,4,48]{3,2,1,0:T(4,128)S(1)} %collective-permute-done.4, f32[2,2]{1,0:T(2,128)S(1)} %bitcast.23, ...), kind=kOutput, calls=%fused_computation.12 | convolution fusion | flops 69342208 | bytes 5949440 | tf_op jit(solution)/shard_map/xfcr,cl->xfrl/dot_general | solution.py:283
  64.1 0.0 collective-permute-done.7.below_ref
  64.1 0.0 collective-permute-done.6.above_ref
  64.1 0.0 copy-done
  64.1 0.0 copy-done.4
  64.1 0.0 copy-done.5
  64.1 32.7 %predict0.1 = (f32[2,16,256,512]{3,2,1,0:T(8,128)}, f32[8,128]{1,0:T(8,128)S(1)}) custom-call(s32[4]{0:T(128)S(1)} %copy-done.4, f32[5]{0:T(128)S(1)} %copy-done.5, f32[2,16,256,512]{3,2,1,0:T(8,128)} %wave_ref.5, f32[256,1]{1,0:T(8,128)S(1)} %copy.9.mask_ref, f32[2,8,48,512]{3,2,1,0:T(8,128)} %collective-permute-done.6.above_ref, ...), custom_call_target="tpu_custom_call" | custom-call | flops 8053063680 | bytes 20971520 | tf_op jit(solution)/shard_map/predict0/pallas_call | solution.py:120
  96.8 0.0 copy-start.2
  96.8 0.0 collective-permute-done.1.below_ref
  96.8 0.0 collective-permute-done.above_ref
  96.8 32.7 %predict8.1 = (f32[2,16,256,512]{3,2,1,0:T(8,128)}, f32[8,128]{1,0:T(8,128)S(1)}) custom-call(s32[4]{0:T(128)S(1)} %copy-done.4, f32[5]{0:T(128)S(1)} %copy-done.5, f32[2,16,256,512]{3,2,1,0:T(8,128)} %wave_ref.5, f32[256,1]{1,0:T(8,128)S(1)} %copy.9.mask_ref, f32[2,8,48,512]{3,2,1,0:T(8,128)S(1)} %collective-permute-done.above_ref, ...), custom_call_target="tpu_custom_call", output_to_operand_aliasing={{0}: (8, {})} | custom-call | flops 8053063680 | bytes 20971520 | tf_op jit(solution)/shard_map/predict8/pallas_call | solution.py:120
  129.5 0.0 copy-done.2
  129.5 0.0 copy-start.3
  129.5 0.6 copy-done.3
  130.1 14.7 %gains1.1.gain_ref = f32[8,128]{1,0:T(8,128)} custom-call(f32[8,128]{1,0:T(8,128)} %copy-done.2, f32[8,128]{1,0:T(8,128)} %copy-done.3), custom_call_target="tpu_custom_call" | custom-call | flops 1000 | bytes 8388608 | tf_op jit(solution)/shard_map/gains1/pallas_call | solution.py:199
  144.8 0.0 copy-start.1
  144.9 0.7 copy-done.1
  145.5 22.2 %subtract0.1 = f32[2,16,256,512]{3,2,1,0:T(8,128)} custom-call(f32[8,128]{1,0:T(8,128)S(1)} %copy-done.1, f32[2,16,256,512]{3,2,1,0:T(8,128)} %wave_ref.5, f32[2,16,256,512]{3,2,1,0:T(8,128)} %get-tuple-element.4.mult_ref), custom_call_target="tpu_custom_call" | custom-call | bytes 50331648 | tf_op jit(solution)/shard_map/subtract0/pallas_call | solution.py:238
  (1 shorter events, 0.0 us)
Async XLA Ops:
  7.7 56.4 %collective-permute-start.7 = (f32[2,8,48,512]{3,2,1,0:T(8,128)}, f32[2,8,48,512]{3,2,1,0:T(8,128)}, u32[]{:S(2)}, u32[]{:S(2)}) collective-permute-start(f32[2,8,48,512]{3,2,1,0:T(8,128)} %get-tuple-element.10), channel_id=1, source_target_pairs={{1,0},{2,1},{3,2},{4,3},{5,4},{6,5},{7,6},{9,8},{10,9},{11,10},{12... | collective-permute-start | bytes 4718600 | tf_op jit(solution)/shard_map/ppermute | solution.py:27
  8.9 55.1 %collective-permute-start.6 = (f32[2,8,48,512]{3,2,1,0:T(8,128)}, f32[2,8,48,512]{3,2,1,0:T(8,128)}, u32[]{:S(2)}, u32[]{:S(2)}) collective-permute-start(f32[2,8,48,512]{3,2,1,0:T(8,128)} %get-tuple-element.15), channel_id=1, source_target_pairs={{0,1},{1,2},{2,3},{3,4},{4,5},{5,6},{6,7},{8,9},{9,10},{10,11},{11... | collective-permute-start | bytes 4718600 | tf_op jit(solution)/shard_map/ppermute | solution.py:27
  17.4 12.5 %collective-permute-start.2 = (f32[2,16,2,256]{3,2,1,0:T(2,128)S(1)}, f32[2,16,2,256]{3,2,1,0:T(2,128)S(1)}, u32[]{:S(2)}, u32[]{:S(2)}) collective-permute-start(f32[2,16,2,256]{3,2,1,0:T(2,128)S(1)} %fusion.7), channel_id=1, source_target_pairs={{8,0},{16,8},{24,16},{9,1},{17,9},{25,17},{10,2},{18,10},{26,18},{... | collective-permute-start | bytes 196616 | tf_op jit(solution)/shard_map/ppermute | solution.py:27
  18.7 78.1 %collective-permute-start.1 = (f32[2,8,48,512]{3,2,1,0:T(8,128)}, f32[2,8,48,512]{3,2,1,0:T(8,128)S(1)}, u32[]{:S(2)}, u32[]{:S(2)}) collective-permute-start(f32[2,8,48,512]{3,2,1,0:T(8,128)} %get-tuple-element.11), channel_id=1, source_target_pairs={{1,0},{2,1},{3,2},{4,3},{5,4},{6,5},{7,6},{9,8},{10,9},{11,10},{12... | collective-permute-start | bytes 4718600 | tf_op jit(solution)/shard_map/ppermute | solution.py:27
  20.0 76.8 %collective-permute-start = (f32[2,8,48,512]{3,2,1,0:T(8,128)}, f32[2,8,48,512]{3,2,1,0:T(8,128)S(1)}, u32[]{:S(2)}, u32[]{:S(2)}) collective-permute-start(f32[2,8,48,512]{3,2,1,0:T(8,128)} %get-tuple-element.14), channel_id=1, source_target_pairs={{0,1},{1,2},{2,3},{3,4},{4,5},{5,6},{6,7},{8,9},{9,10},{10,11},{11... | collective-permute-start | bytes 4718600 | tf_op jit(solution)/shard_map/ppermute | solution.py:27
  29.8 6.6 %collective-permute-start.3 = (f32[2,16,2,256]{3,2,1,0:T(2,128)S(1)}, f32[2,16,2,256]{3,2,1,0:T(2,128)S(1)}, u32[]{:S(2)}, u32[]{:S(2)}) collective-permute-start(f32[2,16,2,256]{3,2,1,0:T(2,128)S(1)} %fusion.13), channel_id=1, source_target_pairs={{0,8},{8,16},{16,24},{1,9},{9,17},{17,25},{2,10},{10,18},{18,26},{... | collective-permute-start | bytes 196616 | tf_op jit(solution)/shard_map/ppermute | solution.py:27
  37.2 3.3 %collective-permute-start.4 = (f32[2,16,4,48]{3,2,1,0:T(4,128)S(1)}, f32[2,16,4,48]{3,2,1,0:T(4,128)S(1)}, u32[]{:S(2)}, u32[]{:S(2)}) collective-permute-start(f32[2,16,4,48]{3,2,1,0:T(4,128)S(1)} %get-tuple-element.16), channel_id=1, source_target_pairs={{0,1},{1,2},{2,3},{3,4},{4,5},{5,6},{6,7},{8,9},{9,10},{10,11},{11... | collective-permute-start | bytes 73736 | tf_op jit(solution)/shard_map/ppermute | solution.py:27
  40.5 12.1 %collective-permute-start.5 = (f32[2,16,4,48]{3,2,1,0:T(4,128)}, f32[2,16,4,48]{3,2,1,0:T(4,128)S(1)}, u32[]{:S(2)}, u32[]{:S(2)}) collective-permute-start(f32[2,16,4,48]{3,2,1,0:T(4,128)} %get-tuple-element.17), channel_id=1, source_target_pairs={{1,0},{2,1},{3,2},{4,3},{5,4},{6,5},{7,6},{9,8},{10,9},{11,10},{12... | collective-permute-start | bytes 73736 | tf_op jit(solution)/shard_map/ppermute | solution.py:27
  42.1 22.0 %copy-start = (f32[2,256,1024]{2,1,0:T(8,128)S(1)}, f32[2,256,1024]{2,1,0:T(8,128)}, u32[]{:S(2)}) copy-start(f32[2,256,1024]{2,1,0:T(8,128)} %band_ref.3) | copy-start | bytes 6291460
  42.1 22.0 %copy-start.4 = (s32[4]{0:T(128)S(1)}, s32[4]{0:T(128)}, u32[]{:S(2)}) copy-start(s32[4]{0:T(128)} %shift_ref.3) | copy-start | bytes 52
  42.1 22.0 %copy-start.5 = (f32[5]{0:T(128)S(1)}, f32[5]{0:T(128)}, u32[]{:S(2)}) copy-start(f32[5]{0:T(128)} %taper_ref.3) | copy-start | bytes 64
  96.8 32.8 %copy-start.2 = (f32[8,128]{1,0:T(8,128)}, f32[8,128]{1,0:T(8,128)S(1)}, u32[]{:S(2)}) copy-start(f32[8,128]{1,0:T(8,128)S(1)} %get-tuple-element.8.refs_0_) | copy-start | bytes 12292
  129.5 0.6 copy-start.3
  144.8 0.7 copy-start.1
